TPU v7x, 16 devices: a whole 2x2x2 slice. The times are simulated.
16 devices in a mesh: dp: 2 (over z), cp: 8 (over y, x, core).
Axes of the slice: x: 2, y: 2, z: 2, core: 2. Of those that a mesh axis runs over, the one named last changes fastest.
Arguments:
- x: bfloat16 [32, 7168], P('dp'), parts along dimension 0
- w_dq: bfloat16 [7168, 1536], replicated
- g_q: float32 [1536], replicated
- w_uq: bfloat16 [1536, 24576], replicated
- w_dkv: bfloat16 [7168, 576], replicated
- g_kv: float32 [512], replicated
- w_uk: bfloat16 [512, 128, 128], replicated
- w_uv: bfloat16 [512, 128, 128], replicated
- w_o: bfloat16 [16384, 7168], replicated
- cache_c: bfloat16 [32, 32768, 512], P('dp', 'cp'), parts along dimension 0
- cache_kr: bfloat16 [32, 32768, 64], P('dp', 'cp'), parts along dimension 0
- ctx_len: int32 [32], P('dp'), parts along dimension 0
Outputs:
- output 1: bfloat16 [32, 7168], P('dp'), parts along dimension 0
- output 2: bfloat16 [32, 512], P('dp'), parts along dimension 0
- output 3: bfloat16 [32, 64], P('dp'), parts along dimension 0
There are 2 independent parts. A program takes and returns all parts, laid end to end along the dimension named above; an argument that names none is the same for every part.
All inputs are finite; a program needn't handle non-finite values.
Results may differ from a plain program's by a relative error of at most 0.0063435.
Values sent between devices are 32-bit elements.
A program may use at most 1.75 GiB of HBM per device.

v0:
```python
import jax
import jax.numpy as jnp
from jax import lax
from jax.sharding import PartitionSpec as P, NamedSharding

NORM_EPS = 1e-6
ROPE_THETA = 10000.0
MASKED = -1e30


def rms_norm(values, gain_vec):
    mean_sq = jnp.mean(jnp.square(values), axis=-1, keepdims=True)
    return values * lax.rsqrt(mean_sq + NORM_EPS) * gain_vec


def rope_tables(positions, rope_dim):
    half_dim = rope_dim // 2
    inv_freq = ROPE_THETA ** (-2.0 * jnp.arange(half_dim, dtype=jnp.float32) / rope_dim)
    angles = positions.astype(jnp.float32)[..., None] * inv_freq
    return jnp.cos(angles), jnp.sin(angles)


def rope_rotate(values, cos_tab, sin_tab):
    half_dim = values.shape[-1] // 2
    lo_half = values[..., :half_dim]
    hi_half = values[..., half_dim:]
    return jnp.concatenate([lo_half * cos_tab - hi_half * sin_tab, hi_half * cos_tab + lo_half * sin_tab], axis=-1)


def project_step(x, w_dq, g_q, w_uq, w_dkv, g_kv, w_uk, ctx_len):
    n_req = x.shape[0]
    latent, n_heads, nope_dim = w_uk.shape
    rope_dim = w_dkv.shape[1] - latent
    cq_low = jnp.dot(x, w_dq, preferred_element_type=jnp.float32).astype(jnp.bfloat16)
    cq_norm = rms_norm(cq_low.astype(jnp.float32), g_q).astype(jnp.bfloat16)
    q_full = jnp.dot(cq_norm, w_uq, preferred_element_type=jnp.float32).astype(jnp.bfloat16)
    q_full = q_full.reshape(n_req, n_heads, nope_dim + rope_dim)
    cos_tab, sin_tab = rope_tables(ctx_len, rope_dim)
    q_rope = rope_rotate(q_full[:, :, nope_dim:].astype(jnp.float32), cos_tab[:, None, :], sin_tab[:, None, :]).astype(jnp.bfloat16)
    q_lat = jnp.einsum('bhn,khn->bhk', q_full[:, :, :nope_dim], w_uk, preferred_element_type=jnp.float32).astype(jnp.bfloat16)
    kv_full = jnp.dot(x, w_dkv, preferred_element_type=jnp.float32)
    c_new = rms_norm(kv_full[:, :latent], g_kv).astype(jnp.bfloat16)
    kr_new = rope_rotate(kv_full[:, latent:], cos_tab, sin_tab).astype(jnp.bfloat16)
    return q_lat, q_rope, c_new, kr_new


def block_partials(q_lat, q_rope, c_new, kr_new, cache_c, cache_kr, ctx_len, shard_idx, score_scale):
    t_dev = cache_c.shape[1]
    scores = (jnp.einsum('bhk,btk->bht', q_lat, cache_c, preferred_element_type=jnp.float32)
              + jnp.einsum('bhr,btr->bht', q_rope, cache_kr, preferred_element_type=jnp.float32)) * score_scale
    positions = shard_idx * t_dev + jnp.arange(t_dev)
    valid_pos = positions[None, None, :] < ctx_len[:, None, None]
    scores = jnp.where(valid_pos, scores, MASKED)
    is_owner = ((ctx_len // t_dev) == shard_idx)[:, None]
    new_score = (jnp.einsum('bhk,bk->bh', q_lat, c_new, preferred_element_type=jnp.float32)
                 + jnp.einsum('bhr,br->bh', q_rope, kr_new, preferred_element_type=jnp.float32)) * score_scale
    new_score = jnp.where(is_owner, new_score, MASKED)
    row_max = jnp.maximum(jnp.max(scores, axis=2), new_score)
    weights = jnp.where(valid_pos, jnp.exp(scores - row_max[:, :, None]), 0.0)
    new_weight = jnp.where(is_owner, jnp.exp(new_score - row_max), 0.0)
    row_sum = jnp.sum(weights, axis=2) + new_weight
    lat_acc = jnp.einsum('bht,btk->bhk', weights.astype(jnp.bfloat16), cache_c, preferred_element_type=jnp.float32)
    lat_acc = lat_acc + new_weight.astype(jnp.bfloat16).astype(jnp.float32)[:, :, None] * c_new.astype(jnp.float32)[:, None, :]
    return row_max, row_sum, lat_acc


def output_step(x, o_lat, w_uv, w_o):
    o_heads = jnp.einsum('bhk,khv->bhv', o_lat, w_uv, preferred_element_type=jnp.float32).astype(jnp.bfloat16)
    attn_out = jnp.dot(o_heads.reshape(x.shape[0], -1), w_o, preferred_element_type=jnp.float32)
    return (x.astype(jnp.float32) + attn_out).astype(jnp.bfloat16)


def solution(mesh):
    def decode_step(x, w_dq, g_q, w_uq, w_dkv, g_kv, w_uk, w_uv, w_o, cache_c, cache_kr, ctx_len):
        score_scale = (w_uk.shape[2] + cache_kr.shape[2]) ** -0.5
        shard_idx = lax.axis_index('cp')
        q_lat, q_rope, c_new, kr_new = project_step(x, w_dq, g_q, w_uq, w_dkv, g_kv, w_uk, ctx_len)
        row_max, row_sum, lat_acc = block_partials(q_lat, q_rope, c_new, kr_new, cache_c, cache_kr, ctx_len, shard_idx, score_scale)
        packed = jnp.concatenate([row_max[:, :, None], row_sum[:, :, None], lat_acc], axis=2)
        gathered = lax.all_gather(packed, 'cp')
        block_max = gathered[:, :, :, 0]
        glob_max = jnp.max(block_max, axis=0)
        factor = jnp.exp(block_max - glob_max[None])
        mass_sum = jnp.sum(factor * gathered[:, :, :, 1], axis=0)
        lat_sum = jnp.sum(factor[:, :, :, None] * gathered[:, :, :, 2:], axis=0)
        o_lat = (lat_sum / mass_sum[:, :, None]).astype(jnp.bfloat16)
        return output_step(x, o_lat, w_uv, w_o), c_new, kr_new

    spec_rows = P('dp', None)
    spec_cache = P('dp', 'cp', None)
    in_specs = (spec_rows, P(), P(), P(), P(), P(), P(), P(), P(), spec_cache, spec_cache, P('dp'))
    out_specs = (spec_rows, spec_rows, spec_rows)
    return jax.shard_map(decode_step, mesh=mesh, in_specs=in_specs, out_specs=out_specs, check_vma=False)
```

profile of v0, /device:TPU:0, one launch (start us, length us, event | category | flops | bytes accessed | tf_op | source)
XLA Modules:
  0.0 534.5 jit_solution(4524993915718865588)
XLA Ops:
  7.2 9.0 %multiply_reduce_fusion = (f32[16]{0:T(128)S(1)}, f32[16,1536]{1,0:T(8,128)S(1)}) fusion(bf16[16,7168]{1,0:T(8,128)(2,1)} %param.12, bf16[7168,1536]{1,0:T(8,128)(2,1)} %param.13), kind=kOutput, calls=%fused_computation.42 | convolution fusion | flops 352419840 | bytes 22347840 | tf_op jit(solution)/shard_map/dot_general | solution.py:34
  16.3 26.4 %convolution_convert_fusion = bf16[16,24576]{1,0:T(8,128)(2,1)S(1)} fusion(bf16[1536,24576]{1,0:T(8,128)(2,1)} %param.15, f32[16,1536]{1,0:T(8,128)S(1)} %get-tuple-element.14, f32[1536]{0:T(1024)S(1)} %copy-done.1, f32[16]{0:T(128)S(1)} %add_rsqrt_fusion.1), kind=kOutput, calls=%fused_computation.6 | convolution fusion | flops 1208426496 | bytes 76388416 | tf_op jit(solution)/shard_map/dot_general | solution.py:36
  42.7 1.2 reshape.119
  43.9 0.1 slice.44
  44.0 0.1 slice.43
  44.2 5.6 %fusion.55 = f32[16,576]{1,0:T(8,128)S(1)} fusion(bf16[16,7168]{1,0:T(8,128)(2,1)S(1)} %copy-done, bf16[7168,576]{0,1:T(8,128)(2,1)} %param.16), kind=kOutput, calls=%fused_computation.81 | convolution fusion | flops 132120576 | bytes 8523776 | tf_op jit(solution)/shard_map/dot_general | solution.py:41
  49.8 0.1 multiply_reduce_fusion.1
  49.9 0.1 broadcast_compare_fusion
  50.0 0.2 copy.58
  50.3 0.1 subtract_convert_fusion.1
  50.5 0.2 subtract_convert_fusion
  50.7 0.2 fusion.38
  50.9 19.0 %fusion.39 = f32[16,128,4096]{2,1,0:T(8,128)} fusion(bf16[16,4096,64]{1,2,0:T(8,128)(2,1)} %param.22, bf16[16,128,32]{1,2,0:T(8,128)(2,1)S(1)} %get-tuple-element.8, bf16[16,128,32]{1,2,0:T(8,128)(2,1)S(1)} %get-tuple-element.7), kind=kOutput, calls=%fused_computation.39 | convolution fusion | flops 1074266112 | bytes 42205184 | tf_op jit(solution)/shard_map/bhr,btr->bht/dot_general | solution.py:50
  70.0 41.1 %convert_bitcast_fusion = bf16[16,128,512]{2,0,1:T(8,128)(2,1)S(1)} fusion(bf16[512,128,128]{2,1,0:T(8,128)(2,1)} %param.18, bf16[16,128,128]{2,1,0:T(8,128)(2,1)S(1)} %slice.43), kind=kOutput, calls=%fused_computation.25 | convolution fusion | flops 269484032 | bytes 19398656 | tf_op jit(solution)/shard_map/bhn,khn->bhk/dot_general | solution.py:40
  111.1 1.2 fusion.21
  112.3 45.3 %fusion.11 = (f32[16,128]{1,0:T(8,128)S(1)}, f32[16,128,4096]{2,1,0:T(8,128)}) fusion(f32[16,128,4096]{2,1,0:T(8,128)} %fusion.39, pred[16,4096]{1,0:T(8,128)(4,1)S(1)} %broadcast_compare_fusion, bf16[16,4096,512]{2,1,0:T(8,128)(2,1)} %param.21, bf16[16,128,512]{2,0,1:T(8,128)(2,1)S(1)} %convert_bitcast_fusion), kind=kOutput, calls=%fused_computation.14 | convolution fusion | flops 8623486976 | bytes 136388608 | tf_op jit(solution)/shard_map/bhk,btk->bht/dot_general | solution.py:49
  157.7 22.7 %fusion.2 = f32[16,128]{1,0:T(8,128)S(1)} fusion(f32[16,128]{1,0:T(8,128)S(1)} %fusion.47, f32[16,128,4096]{2,1,0:T(8,128)} %get-tuple-element.16, f32[16,128,4096]{2,1,0:T(8,128)} %fusion.39, pred[16,4096]{1,0:T(8,128)(4,1)S(1)} %broadcast_compare_fusion), kind=kLoop, calls=%fused_computation.5 | loop fusion | flops 50329600 | bytes 67190784 | tf_op jit(solution)/shard_map/reduce_sum | solution.py:61
  180.5 0.4 copy.46
  180.9 0.4 copy.45
  181.3 44.3 %multiply_add_fusion = f32[16,128,512]{2,1,0:T(8,128)} fusion(f32[16,512]{1,0:T(8,128)S(1)} %get-tuple-element.5, f32[16,128]{1,0:T(8,128)S(1)} %convert_element_type.97, bf16[16,4096,512]{2,1,0:T(8,128)(2,1)} %param.21, f32[16,128]{1,0:T(8,128)S(1)} %fusion.47, f32[16,128,4096]{2,1,0:T(8,128)} %get-tuple-element.16, f32[16,128,4096]{2,1,0:T(8,128)} %fusion.39, ...), kind=kOutput, calls=%fused_computation.21 | convolution fusion | flops 8642363392 | bytes 138526720 | tf_op jit(solution)/shard_map/bht,btk->bhk/dot_general | solution.py:62
  225.6 6.5 %pad_maximum_fusion = f32[16,128,514]{2,1,0:T(8,128)} fusion(f32[16,128,512]{2,1,0:T(8,128)} %multiply_add_fusion, f32[16,128,1]{2,1,0:T(8,128)S(1)} %copy.46, f32[16,128,1]{2,1,0:T(8,128)S(1)} %copy.45), kind=kLoop, calls=%fused_computation.19 | loop fusion | flops 2105344 | bytes 8421376 | tf_op jit(solution)/shard_map/concatenate | solution.py:79
  232.0 6.0 %copy.47 = f32[16,128,514]{1,0,2:T(8,128)} copy(f32[16,128,514]{2,1,0:T(8,128)} %pad_maximum_fusion) | data formatting | bytes 8421376 | tf_op jit(solution)/shard_map/concatenate | solution.py:79
  238.0 0.7 pad_maximum_fusion.4
  238.7 167.9 %all-gather.3.cloned.1.call-done = f32[128,128,514]{1,0,2:T(8,128)} async-done(((f32[16,128,514]{1,0,2:T(8,128)}), f32[128,128,514]{1,0,2:T(8,128)}) %all-gather.3.cloned.1.call-update) | async-done | bytes 33685520 | tf_op jit(solution)/shard_map/all_gather | solution.py:80
  406.6 0.9 slice_reduce_fusion
  407.4 0.9 fusion.41
  408.3 0.9 exponential_bitcast_fusion
  409.2 15.7 %fusion = f32[16,128,512]{1,0,2:T(8,128)} fusion(f32[8,16,128,514]{2,1,0,3:T(8,128)} %bitcast.46, f32[8,16,128]{2,1,0:T(8,128)S(1)} %exponential_bitcast_fusion), kind=kLoop, calls=%fused_computation.1 | loop fusion | flops 15728640 | bytes 37814272 | tf_op jit(solution)/shard_map/reduce_sum | solution.py:85
  424.9 5.3 copy.56
  430.2 2.6 divide_convert_fusion
  432.8 21.3 %fusion.30 = bf16[128,2,8,128]{3,2,1,0:T(8,128)(2,1)S(1)} fusion(bf16[512,128,128]{2,1,0:T(8,128)(2,1)} %param.19, bf16[16,128,512]{2,1,0:T(8,128)(2,1)S(1)} %divide_convert_fusion), kind=kOutput, calls=%fused_computation.31 | convolution fusion | flops 268697600 | bytes 19398656 | tf_op jit(solution)/shard_map/bhk,khv->bhv/dot_general | solution.py:68
  454.1 73.0 %fusion.14 = bf16[16,7168]{1,0:T(8,128)(2,1)} fusion(bf16[16384,7168]{1,0:T(8,128)(2,1)} %param.20, bf16[128,2,8,128]{3,2,1,0:T(8,128)(2,1)S(1)} %fusion.30, bf16[16,7168]{1,0:T(8,128)(2,1)S(1)} %copy-done), kind=kOutput, calls=%fused_computation.18 | convolution fusion | flops 3758440448 | bytes 235864064 | tf_op jit(solution)/shard_map/dot_general | solution.py:69
  (24 shorter events, 0.5 us)
Async XLA Ops:
  7.2 9.1 %copy-start.1 = (f32[1536]{0:T(1024)S(1)}, f32[1536]{0:T(1024)}, u32[]{:S(2)}) copy-start(f32[1536]{0:T(1024)} %param.14) | copy-start | bytes 18436
  7.2 399.4 %all-gather.3.cloned.1.call-start = ((), (), s32[]{:S(2)}) async-start(), calls=%async_computation | async-start | bytes 37896192 | tf_op jit(solution)/shard_map/all_gather | solution.py:80
  16.3 27.9 %copy-start.4 = (s32[16]{0:T(128)S(1)}, s32[16]{0:T(128)}, u32[]{:S(2)}) copy-start(s32[16]{0:T(128)} %param.23) | copy-start | bytes 196
  16.3 27.9 %copy-start = (bf16[16,7168]{1,0:T(8,128)(2,1)S(1)}, bf16[16,7168]{1,0:T(8,128)(2,1)}, u32[]{:S(2)}) copy-start(bf16[16,7168]{1,0:T(8,128)(2,1)} %param.12) | copy-start | bytes 688132
  50.9 19.0 %copy-start.3 = (f32[512]{0:T(512)S(1)}, f32[512]{0:T(512)}, u32[]{:S(2)}) copy-start(f32[512]{0:T(512)} %param.17) | copy-start | bytes 6148
  70.0 87.6 %copy-start.2 = (bf16[16,512]{1,0:T(8,128)(2,1)}, bf16[16,512]{1,0:T(8,128)(2,1)S(1)}, u32[]{:S(2)}) copy-start(bf16[16,512]{1,0:T(8,128)(2,1)S(1)} %get-tuple-element.6) | copy-start | bytes 49156
Sparse Core Ops, SparseCore 0:
  238.1 168.3 all-gather.2
where the time goes:
time: 539 us; the launch traced here: 534 us
  matrix products  286 us (53%)
  waiting for transfers between devices  168 us (31%)
  other arithmetic  51.7 us (10%)
  between operations  14.7 us (3%)
  local copies, waits for them, and re-layouts  13.6 us (3%)
    all_gather x1, waiting for transfers between devices, decode_step(): gathered = lax.all_gather(packed, 'cp')  168 us
    dot_general x1, matrix products, output_step(): jnp.dot(o_heads.reshape(x.shape[0], -1), w_o, preferred_element_type=jnp....  73 us
    dot_general x1, matrix products, block_partials(): jnp.einsum('bhk,btk->bht', q_lat, cache_c, preferred_element_type=jnp.flo...  45.3 us
    dot_general x1, matrix products, block_partials(): jnp.einsum('bht,btk->bhk', weights.astype(jnp.bfloat16), cache_c, preferr...  44.3 us
    dot_general x1, matrix products, project_step(): jnp.einsum('bhn,khn->bhk', q_full[:, :, :nope_dim], w_uk, preferred_eleme...  41.1 us
    dot_general x1, matrix products, project_step(): jnp.dot(cq_norm, w_uq, preferred_element_type=jnp.float32)  26.4 us
    reduce_sum x1, other arithmetic, block_partials(): row_sum = jnp.sum(weights, axis=2) + new_weight  22.7 us
    dot_general x1, matrix products, output_step(): jnp.einsum('bhk,khv->bhv', o_lat, w_uv, preferred_element_type=jnp.float32)  21.3 us
  transfers between devices with their start and end apart: 1, of which 1 were waited for; matrix products, arithmetic and copies ran while one was open for 0% of the time, Pallas kernels for 0%

commit v1 on v0

v1 whole, which is shorter than its diff:
```python
import functools

import jax
import jax.numpy as jnp
from jax import lax
from jax.experimental import pallas as pl
from jax.experimental.pallas import tpu as pltpu
from jax.sharding import PartitionSpec as P

NORM_EPS = 1e-6
ROPE_THETA = 10000.0
MASKED = -1e30
FLOOR = -1e29
LOG2E = 1.4426950408889634


def rms_norm(values, gain_vec):
    mean_sq = jnp.mean(jnp.square(values), axis=-1, keepdims=True)
    return values * lax.rsqrt(mean_sq + NORM_EPS) * gain_vec


def rope_tables(positions, rope_dim):
    half_dim = rope_dim // 2
    inv_freq = ROPE_THETA ** (-2.0 * jnp.arange(half_dim, dtype=jnp.float32) / rope_dim)
    angles = positions.astype(jnp.float32)[..., None] * inv_freq
    return jnp.cos(angles), jnp.sin(angles)


def rope_rotate(values, cos_tab, sin_tab):
    half_dim = values.shape[-1] // 2
    lo_half = values[..., :half_dim]
    hi_half = values[..., half_dim:]
    return jnp.concatenate([lo_half * cos_tab - hi_half * sin_tab, hi_half * cos_tab + lo_half * sin_tab], axis=-1)


def project_step(x, w_dq, g_q, w_uq, w_dkv, g_kv, w_uk, ctx_len):
    n_req = x.shape[0]
    latent, n_heads, nope_dim = w_uk.shape
    rope_dim = w_dkv.shape[1] - latent
    cq_low = jnp.dot(x, w_dq, preferred_element_type=jnp.float32).astype(jnp.bfloat16)
    cq_norm = rms_norm(cq_low.astype(jnp.float32), g_q).astype(jnp.bfloat16)
    q_full = jnp.dot(cq_norm, w_uq, preferred_element_type=jnp.float32).astype(jnp.bfloat16)
    q_full = q_full.reshape(n_req, n_heads, nope_dim + rope_dim)
    cos_tab, sin_tab = rope_tables(ctx_len, rope_dim)
    q_rope = rope_rotate(q_full[:, :, nope_dim:].astype(jnp.float32), cos_tab[:, None, :], sin_tab[:, None, :]).astype(jnp.bfloat16)
    q_lat = jnp.einsum('bhn,khn->bhk', q_full[:, :, :nope_dim], w_uk, preferred_element_type=jnp.float32).astype(jnp.bfloat16)
    kv_full = jnp.dot(x, w_dkv, preferred_element_type=jnp.float32)
    c_new = rms_norm(kv_full[:, :latent], g_kv).astype(jnp.bfloat16)
    kr_new = rope_rotate(kv_full[:, latent:], cos_tab, sin_tab).astype(jnp.bfloat16)
    return q_lat, q_rope, c_new, kr_new


def attend_body(scale, t_chunk, ctx_ref, q_ref, qr_ref, c_ref, kr_ref, acc_ref, ml_ref, s_ref):
    b = pl.program_id(0)
    t_dev = c_ref.shape[1]
    base = lax.axis_index('cp') * t_dev
    limit = ctx_ref[b] - base
    q = q_ref[0]
    qr = qr_ref[0]
    n_chunks = t_dev // t_chunk
    lane_max = None
    nt = (((1,), (1,)), ((), ()))
    for i in range(n_chunks):
        sl = pl.ds(i * t_chunk, t_chunk)
        s = lax.dot_general(q, c_ref[0, sl, :], nt, preferred_element_type=jnp.float32)
        s = s + jnp.dot(qr, kr_ref[0, :, sl], preferred_element_type=jnp.float32)
        pos = lax.broadcasted_iota(jnp.int32, (1, t_chunk), 1) + i * t_chunk
        s = jnp.where(pos < limit, s, MASKED)
        s_ref[:, sl] = s
        cm = jnp.max(s, axis=1, keepdims=True)
        lane_max = cm if lane_max is None else jnp.maximum(lane_max, cm)
    m = jnp.maximum(lane_max, FLOOR)
    k2 = scale * LOG2E
    acc = None
    l = None
    for i in range(n_chunks):
        sl = pl.ds(i * t_chunk, t_chunk)
        p = jnp.exp2((s_ref[:, sl] - m) * k2)
        ls = jnp.sum(p, axis=1, keepdims=True)
        l = ls if l is None else l + ls
        o = jnp.dot(p.astype(jnp.bfloat16), c_ref[0, sl, :], preferred_element_type=jnp.float32)
        acc = o if acc is None else acc + o
    acc_ref[0] = acc
    lane = lax.broadcasted_iota(jnp.int32, (acc.shape[0], 128), 1)
    ml_ref[0] = jnp.where(lane == 0, m * scale, l)


def attend(q_lat, q_rope, cache_c, cache_kr_t, ctx_len, scale):
    n_req, heads, latent = q_lat.shape
    t_dev = cache_c.shape[1]
    rope = q_rope.shape[2]
    grid_spec = pltpu.PrefetchScalarGridSpec(
        num_scalar_prefetch=1,
        grid=(n_req,),
        in_specs=[
            pl.BlockSpec((1, heads, latent), lambda b, c: (b, 0, 0)),
            pl.BlockSpec((1, heads, rope), lambda b, c: (b, 0, 0)),
            pl.BlockSpec((1, t_dev, latent), lambda b, c: (b, 0, 0)),
            pl.BlockSpec((1, rope, t_dev), lambda b, c: (b, 0, 0)),
        ],
        out_specs=[
            pl.BlockSpec((1, heads, latent), lambda b, c: (b, 0, 0)),
            pl.BlockSpec((1, heads, 128), lambda b, c: (b, 0, 0)),
        ],
        scratch_shapes=[pltpu.VMEM((heads, t_dev), jnp.float32)],
    )
    return pl.pallas_call(
        functools.partial(attend_body, scale, min(512, t_dev)),
        grid_spec=grid_spec,
        out_shape=[
            jax.ShapeDtypeStruct((n_req, heads, latent), jnp.float32),
            jax.ShapeDtypeStruct((n_req, heads, 128), jnp.float32),
        ],
        compiler_params=pltpu.CompilerParams(vmem_limit_bytes=60 * 1024 * 1024),
        name='attend',
    )(ctx_len, q_lat, q_rope, cache_c, cache_kr_t)


def solution(mesh):
    n_cp = mesh.shape['cp']

    def decode_step(x, w_dq, g_q, w_uq, w_dkv, g_kv, w_uk, w_uv, w_o, cache_c, cache_kr, ctx_len):
        scale = (w_uk.shape[2] + cache_kr.shape[2]) ** -0.5
        me = lax.axis_index('cp')
        n_heads = w_uk.shape[1]
        hs = n_heads // n_cp
        q_lat, q_rope, c_new, kr_new = project_step(x, w_dq, g_q, w_uq, w_dkv, g_kv, w_uk, ctx_len)
        acc, ml = attend(q_lat, q_rope, cache_c, jnp.swapaxes(cache_kr, 1, 2), ctx_len, scale)
        m, l = ml[:, :, 0], ml[:, :, 1]
        new_s = (jnp.einsum('bhk,bk->bh', q_lat, c_new, preferred_element_type=jnp.float32)
                 + jnp.einsum('bhr,br->bh', q_rope, kr_new, preferred_element_type=jnp.float32)) * scale
        ml_all = lax.all_gather(ml[:, :, :2], 'cp')
        top = jnp.maximum(jnp.max(ml_all[..., 0], axis=0), new_s)
        w_new = jnp.exp(new_s - top)
        total = jnp.sum(jnp.exp(ml_all[..., 0] - top[None]) * ml_all[..., 1], axis=0) + w_new
        part = acc * jnp.exp(m - top)[:, :, None]
        mine = lax.psum_scatter(part, 'cp', scatter_dimension=1, tiled=True)
        w_new = lax.dynamic_slice_in_dim(w_new, me * hs, hs, 1)
        total = lax.dynamic_slice_in_dim(total, me * hs, hs, 1)
        mine = mine + w_new[:, :, None] * c_new.astype(jnp.float32)[:, None, :]
        o_lat = (mine / total[:, :, None]).astype(jnp.bfloat16)
        uv = lax.dynamic_slice_in_dim(w_uv, me * hs, hs, 1)
        o_heads = jnp.einsum('bhk,khv->bhv', o_lat, uv, preferred_element_type=jnp.float32).astype(jnp.bfloat16)
        rows = hs * w_uv.shape[2]
        wo = lax.dynamic_slice_in_dim(w_o, me * rows, rows, 0)
        part_out = jnp.dot(o_heads.reshape(x.shape[0], -1), wo, preferred_element_type=jnp.float32)
        attn_out = lax.psum(part_out, 'cp')
        return (x.astype(jnp.float32) + attn_out).astype(jnp.bfloat16), c_new, kr_new

    spec_rows = P('dp', None)
    spec_cache = P('dp', 'cp', None)
    in_specs = (spec_rows, P(), P(), P(), P(), P(), P(), P(), P(), spec_cache, spec_cache, P('dp'))
    out_specs = (spec_rows, spec_rows, spec_rows)
    return jax.shard_map(decode_step, mesh=mesh, in_specs=in_specs, out_specs=out_specs, check_vma=False)
```

time: 539 us -> 285 us (0.53)
  matrix products: 286 us -> 96.5 us
  waiting for transfers between devices: 168 us -> 89.6 us
  Pallas kernels: 0 us -> 49.1 us
  other arithmetic: 51.7 us -> 9.57 us
  blocking collectives: 0 us -> 10.9 us
    dot_general x7 -> x4, matrix products: 204 us -> 14 us  [the longest x1 12.2 us: decode_step(): jnp.dot(o_heads.reshape(x.shape[0], -1), wo, preferred_element_type=jnp.f...]
    all_gather x1 -> x0, waiting for transfers between devices: 168 us -> none  [decode_step(): gathered = lax.all_gather(packed, 'cp')]
    pallas_call x0 -> x1, Pallas kernels: none -> 49.1 us  [attend(): pl.pallas_call(functools.partial(attend_body, scale, min(512, t_dev)), gr...]
    psum x0 -> x1, waiting for transfers between devices: none -> 46.3 us  [decode_step(): attn_out = lax.psum(part_out, 'cp')]
    reduce_scatter x0 -> x1, waiting for transfers between devices: none -> 43.3 us  [decode_step(): mine = lax.psum_scatter(part, 'cp', scatter_dimension=1, tiled=True)]
    reduce_sum x3 -> x1, other arithmetic: 39.4 us -> 0.02 us  [decode_step(): jnp.sum(jnp.exp(ml_all[..., 0] - top[None]) * ml_all[..., 1], axis=0)]
    all_gather x0 -> x1, blocking collectives: none -> 10.9 us  [decode_step(): ml_all = lax.all_gather(ml[:, :, :2], 'cp')]
    concatenate x1 -> x0, other arithmetic: 6.45 us -> none  [decode_step(): jnp.concatenate([row_max[:, :, None], row_sum[:, :, None], lat_acc], axis=2)]
  transfers between devices with their start and end apart: 1 -> 2, of which waited for: 1 -> 2; matrix products, arithmetic and copies ran while one was open for 0% -> 1% of each run, Pallas kernels for 0% -> 0%
where the time goes in v1:
time: 285 us; the launch traced here: 280 us
  matrix products  96.5 us (34%)
  waiting for transfers between devices  89.6 us (31%)
  Pallas kernels  49.1 us (17%)
  between operations  14.4 us (5%)
  blocking collectives  10.9 us (4%)
  local copies, waits for them, and re-layouts  10 us (4%)
  other arithmetic  9.57 us (3%)
    pallas_call x1, Pallas kernels, attend(): pl.pallas_call(functools.partial(attend_body, scale, min(512, t_dev)), gr...  49.1 us
    psum x1, waiting for transfers between devices, decode_step(): attn_out = lax.psum(part_out, 'cp')  46.3 us
    reduce_scatter x1, waiting for transfers between devices, decode_step(): mine = lax.psum_scatter(part, 'cp', scatter_dimension=1, tiled=True)  43.3 us
    dot_general x1, matrix products, project_step(): jnp.einsum('bhn,khn->bhk', q_full[:, :, :nope_dim], w_uk, preferred_eleme...  41.3 us
    dot_general x1, matrix products, project_step(): jnp.dot(cq_norm, w_uq, preferred_element_type=jnp.float32)  26.7 us
    dot_general x1, matrix products, decode_step(): jnp.dot(o_heads.reshape(x.shape[0], -1), wo, preferred_element_type=jnp.f...  12.2 us
    all_gather x1, blocking collectives, decode_step(): ml_all = lax.all_gather(ml[:, :, :2], 'cp')  10.9 us
    dot_general x1, matrix products, project_step(): jnp.dot(x, w_dq, preferred_element_type=jnp.float32).astype(jnp.bfloat16)  8.99 us
  transfers between devices with their start and end apart: 2, of which 2 were waited for; matrix products, arithmetic and copies ran while one was open for 1% of the time, Pallas kernels for 0%

profile of v1, /device:TPU:0, one launch (start us, length us, event | category | flops | bytes accessed | tf_op | source)
XLA Modules:
  0.0 280.3 jit_solution(13731388068205448634)
XLA Ops:
  7.2 9.0 %multiply_reduce_fusion = (f32[16]{0:T(128)S(1)}, f32[16,1536]{1,0:T(8,128)S(1)}) fusion(bf16[16,7168]{1,0:T(8,128)(2,1)} %param.12, bf16[7168,1536]{1,0:T(8,128)(2,1)} %param.13), kind=kOutput, calls=%fused_computation.24 | convolution fusion | flops 352419840 | bytes 22347840 | tf_op jit(solution)/shard_map/dot_general | solution.py:40
  16.3 26.7 %convolution_convert_fusion = bf16[16,24576]{1,0:T(8,128)(2,1)S(1)} fusion(bf16[1536,24576]{1,0:T(8,128)(2,1)} %param.15, f32[16,1536]{1,0:T(8,128)S(1)} %get-tuple-element.20, f32[1536]{0:T(1024)S(1)} %copy-done.4, f32[16]{0:T(128)S(1)} %add_rsqrt_fusion.1), kind=kOutput, calls=%fused_computation.2 | convolution fusion | flops 1208426496 | bytes 76388416 | tf_op jit(solution)/shard_map/dot_general | solution.py:42
  43.0 1.2 reshape.85
  44.2 0.1 slice_convert_fusion
  44.3 0.9 slice.48
  45.2 5.6 %fusion.31 = f32[16,576]{1,0:T(8,128)S(1)} fusion(bf16[16,7168]{1,0:T(8,128)(2,1)S(1)} %copy-done.2, bf16[7168,576]{0,1:T(8,128)(2,1)} %param.16), kind=kOutput, calls=%fused_computation.58 | convolution fusion | flops 132120576 | bytes 8523776 | tf_op jit(solution)/shard_map/dot_general | solution.py:47
  50.8 41.3 %fusion.2 = bf16[128,16,512]{2,1,0:T(8,128)(2,1)S(1)} fusion(bf16[512,128,128]{2,1,0:T(8,128)(2,1)} %param.18, bf16[16,128,128]{2,1,0:T(8,128)(2,1)} %slice.48), kind=kOutput, calls=%fused_computation.3 | convolution fusion | flops 268435456 | bytes 19398656 | tf_op jit(solution)/shard_map/bhn,khn->bhk/dot_general | solution.py:46
  92.1 2.5 copy.67
  94.5 0.1 multiply_reduce_fusion.1
  94.7 0.1 subtract_convert_fusion.1
  94.8 0.5 subtract_convert_fusion
  95.3 0.3 pad_maximum_fusion.qr_ref
  95.6 0.1 fusion.39
  95.7 0.4 fusion.25
  96.0 0.3 copy-done.1
  96.4 49.1 %attend.1 = (f32[16,128,512]{2,1,0:T(8,128)}, f32[16,128,128]{2,1,0:T(8,128)}) custom-call(s32[16]{0:T(128)} %ctx_ref.1, bf16[16,128,512]{2,1,0:T(8,128)(2,1)} %bitcast.38, bf16[16,128,64]{2,1,0:T(8,128)(2,1)} %copy-done.1, bf16[16,4096,512]{2,1,0:T(8,128)(2,1)} %c_ref.1, bf16[16,64,4096]{2,1,0:T(8,128)(2,1)} %bitcast.40), custom_call_target="tpu_custom_call" | custom-call | tf_op jit(solution)/shard_map/attend/pallas_call | solution.py:107
  145.5 1.6 slice_reduce_fusion
  147.0 1.6 copy.33
  148.6 10.9 %all-gather = f32[128,128,2]{1,2,0:T(2,128)S(1)} all-gather(f32[16,128,2]{1,2,0:T(2,128)S(1)} %copy.33), channel_id=2, replica_groups=mesh['dp'=2,'cp'=8] {'cp'}, dimensions={0}, use_global_device_ids=true | all-gather | bytes 147456 | tf_op jit(solution)/shard_map/all_gather | solution.py:132
  159.6 0.1 fusion.29
  159.7 0.6 fusion.23
  160.3 4.5 %broadcast_multiply_fusion = f32[16,128,512]{2,1,0:T(8,128)} fusion(f32[16,128,512]{2,1,0:T(8,128)} %get-tuple-element.5, f32[16,128]{1,0:T(8,128)S(1)} %subtract_exponential_fusion.1), kind=kLoop, calls=%fused_computation.11 | loop fusion | flops 1048576 | bytes 8396800 | tf_op jit(solution)/shard_map/mul | solution.py:136
  164.9 0.0 all-reduce.2.cloned.1.call-start
  165.0 0.1 constant_dynamic-slice_fusion
  165.0 2.0 constant_dynamic-slice_fusion.1
  167.0 43.3 %reduce-scatter.2.cloned.1.call-done = f32[16,16,512]{2,1,0:T(8,128)} async-done(((f32[16,128,512]{2,1,0:T(8,128)}), f32[16,16,512]{2,1,0:T(8,128)}) %reduce-scatter.2.cloned.1.call-update) | async-done | bytes 524304 | tf_op jit(solution)/shard_map/reduce_scatter | solution.py:137
  210.3 1.2 divide_convert_fusion
  211.5 0.8 fusion.11
  212.3 12.2 %fusion = f32[16,7168]{1,0:T(8,128)} fusion(bf16[16384,7168]{1,0:T(8,128)(2,1)} %param.20, s32[]{:T(128)S(6)} %select_n.9, bf16[16,2,8,128]{3,2,1,0:T(8,128)(2,1)S(1)} %fusion.11), kind=kOutput, calls=%fused_computation | convolution fusion | flops 469762048 | bytes 29884420 | tf_op jit(solution)/shard_map/dot_general | solution.py:146
  224.5 0.7 pad_maximum_fusion.1
  225.2 46.3 %all-reduce.2.cloned.1.call-done = f32[16,7168]{1,0:T(8,128)} async-done(((f32[16,7168]{1,0:T(8,128)}), f32[16,7168]{1,0:T(8,128)}) %all-reduce.2.cloned.1.call-update) | async-done | bytes 458768 | tf_op jit(solution)/shard_map/psum | solution.py:147
  271.5 1.7 add_convert_fusion.1
  (25 shorter events, 0.2 us)
Async XLA Ops:
  7.2 203.2 %reduce-scatter.2.cloned.1.call-start = ((), (), s32[]{:S(2)}) async-start(), calls=%async_computation.1 | async-start | bytes 4718592 | tf_op jit(solution)/shard_map/reduce_scatter | solution.py:137
  7.2 9.0 %copy-start.4 = (f32[1536]{0:T(1024)S(1)}, f32[1536]{0:T(1024)}, u32[]{:S(2)}) copy-start(f32[1536]{0:T(1024)} %param.14) | copy-start | bytes 18436
  16.2 28.9 %copy-start.2 = (bf16[16,7168]{1,0:T(8,128)(2,1)S(1)}, bf16[16,7168]{1,0:T(8,128)(2,1)}, u32[]{:S(2)}) copy-start(bf16[16,7168]{1,0:T(8,128)(2,1)} %param.12) | copy-start | bytes 688132
  43.0 7.8 %copy-start.6 = (s32[16]{0:T(128)S(1)}, s32[16]{0:T(128)}, u32[]{:S(2)}) copy-start(s32[16]{0:T(128)} %ctx_ref.1) | copy-start | bytes 196
  95.6 0.8 copy-start.1
  96.4 63.2 %copy-start.5 = (f32[512]{0:T(512)S(1)}, f32[512]{0:T(512)}, u32[]{:S(2)}) copy-start(f32[512]{0:T(512)} %param.17) | copy-start | bytes 6148
  96.4 63.3 %copy-start = (bf16[128,16,512]{2,0,1:T(8,128)(2,1)S(1)}, bf16[128,16,512]{2,0,1:T(8,128)(2,1)}, u32[]{:S(2)}) copy-start(bf16[128,16,512]{2,0,1:T(8,128)(2,1)} %copy.67) | copy-start | bytes 6291460
  159.6 7.4 %copy-start.3 = (bf16[16,512]{1,0:T(8,128)(2,1)}, bf16[16,512]{1,0:T(8,128)(2,1)S(1)}, u32[]{:S(2)}) copy-start(bf16[16,512]{1,0:T(8,128)(2,1)S(1)} %get-tuple-element.8) | copy-start | bytes 49156
  164.9 106.6 %all-reduce.2.cloned.1.call-start = ((), (), s32[]{:S(2)}) async-start(), calls=%async_computation.2 | async-start | bytes 917504 | tf_op jit(solution)/shard_map/psum | solution.py:147
Sparse Core Ops, SparseCore 0:
  165.0 45.2 reduce-scatter.1
  224.6 46.8 all-reduce.1
